TPU v7x, 32 devices: a whole 2x2x4 slice. The times are simulated.
32 devices in a mesh: rows: 32 (over z, y, x, core).
Axes of the slice: x: 2, y: 2, z: 4, core: 2. Of those that a mesh axis runs over, the one named last changes fastest.
Arguments:
- right_sides: float32 [32, 32768], P(None, 'rows'), may hold values from -48 to 48
- initial: float32 [32, 32768], P(None, 'rows'), may hold values from -1.2 to 1.2
- diag_blocks: float32 [32768, 256], P('rows'), may hold values from -2 to 9
- sub_blocks: float32 [32768, 256], P('rows'), may hold values from -0.21875 to 0.21875
- super_blocks: float32 [32768, 256], P('rows'), may hold values from -0.21875 to 0.21875
- local_inverse: bfloat16 [32768, 1024], P('rows'), may hold values from -1 to 1
- upper_spikes: bfloat16 [256, 32768], P(None, 'rows'), may hold values from -0.21875 to 0.21875
- lower_spikes: bfloat16 [256, 32768], P(None, 'rows'), may hold values from -2 to 2
Outputs:
- solution: float32 [32, 32768], P(None, 'rows')
- residual_norms: float32 [3, 32], replicated
All inputs are finite; a program needn't handle non-finite values.
Results may differ from a plain program's by a relative error of at most 0.002.
The roundings to bfloat16 on the way count: a program that leaves them out, or rounds other values in their place, can miss the bound.
Values may be sent and summed in bfloat16 or wider, within the bound.
A program may use at most 64 MiB of HBM per device.

v0:
```python
import jax
import jax.numpy as jnp
from jax import lax
from jax.sharding import PartitionSpec as P

ITERS = 2


maximum_level = lax.Precision.HIGHEST


def with_halo(block, sides, width):
    for axis, dim in sides:
        count = lax.axis_size(axis)
        forward = [(i, i + 1) for i in range(count - 1)]
        backward = [(target, source) for source, target in forward]
        low = lax.ppermute(
            lax.slice_in_dim(block, block.shape[dim] - width, None, axis=dim), axis, forward
        )
        high = lax.ppermute(lax.slice_in_dim(block, 0, width, axis=dim), axis, backward)
        block = jnp.concatenate([low, block, high], axis=dim)
    return block


def shifted(block, axis, distance):
    devices = range(lax.axis_size(axis))
    route = [(i - distance, i) for i in devices if i - distance in devices]
    return lax.ppermute(block, axis, route)


def split_blocks(matrix, band_width):
    return matrix.reshape(matrix.shape[0] // band_width, band_width, band_width)


def residual_of(right_sides, solution, diag_mat, lower_mat, upper_mat, band_width):
    padded = with_halo(solution, (("rows", 1),), band_width)
    block_count = diag_mat.shape[0]
    stacked = padded.reshape(padded.shape[0], block_count + 2, band_width)
    applied = jnp.einsum("rkb,kbc->rkc", stacked[:, 1:-1], diag_mat, precision=maximum_level)
    applied = applied + jnp.einsum(
        "rkb,kbc->rkc", stacked[:, :-2], lower_mat, precision=maximum_level
    )
    applied = applied + jnp.einsum(
        "rkb,kbc->rkc", stacked[:, 2:], upper_mat, precision=maximum_level
    )
    return right_sides - applied.reshape(right_sides.shape)


def body(
    right_sides,
    initial,
    diag_blocks,
    sub_blocks,
    super_blocks,
    local_inverse,
    upper_spikes,
    lower_spikes,
):
    band_width = diag_blocks.shape[1]
    diag_mat = split_blocks(diag_blocks, band_width)
    lower_mat = split_blocks(sub_blocks, band_width)
    upper_mat = split_blocks(super_blocks, band_width)
    chain_mat = -lower_spikes[:, -band_width:].astype(jnp.float32)
    bottom_upper = upper_spikes[:, -band_width:].astype(jnp.float32)
    order_total = right_sides.shape[1] * lax.axis_size("rows")
    own_lower = lower_spikes[:, :band_width].astype(jnp.float32)
    level_depth = (lax.axis_size("rows") - 1).bit_length()
    moving = shifted(chain_mat, "rows", 1)
    level_mats = [moving]
    for level_index in range(level_depth - 1):
        arrived = shifted(moving, "rows", 1 << level_index)
        moving = jnp.matmul(arrived, moving, precision=maximum_level)
        level_mats.append(moving)
    records = []

    def record_norm(residual):
        partial_sum = jnp.sum(residual * residual, axis=1)
        records.append(lax.psum(partial_sum, "rows"))

    solution = initial
    for turn_index in range(ITERS):
        residual = residual_of(right_sides, solution, diag_mat, lower_mat, upper_mat, band_width)
        record_norm(residual)
        rounded = residual.astype(jnp.bfloat16)
        local_part = jnp.dot(rounded, local_inverse, preferred_element_type=jnp.float32)
        own_top = local_part[:, :band_width]
        next_top = shifted(own_top, "rows", -1)
        offset = local_part[:, -band_width:] - jnp.matmul(
            next_top, bottom_upper, precision=maximum_level
        )
        moving_sum = shifted(offset, "rows", 1)
        for level_index in range(level_depth):
            arrived_sum = shifted(moving_sum, "rows", 1 << level_index)
            moving_sum = (
                jnp.matmul(arrived_sum, level_mats[level_index], precision=maximum_level)
                + moving_sum
            )
        mine_tip = own_top - jnp.matmul(moving_sum, own_lower, precision=maximum_level)
        top_tip = shifted(mine_tip, "rows", -1)
        correction = local_part - jnp.dot(
            top_tip.astype(jnp.bfloat16), upper_spikes, preferred_element_type=jnp.float32
        )
        correction = correction - jnp.dot(
            moving_sum.astype(jnp.bfloat16), lower_spikes, preferred_element_type=jnp.float32
        )
        solution = solution + correction
    residual = residual_of(right_sides, solution, diag_mat, lower_mat, upper_mat, band_width)
    record_norm(residual)
    totals = jnp.stack(records)
    return (solution, jnp.sqrt(totals / order_total))


def solution(mesh):
    return jax.shard_map(
        body,
        mesh=mesh,
        in_specs=(
            P(None, "rows"),
            P(None, "rows"),
            P("rows", None),
            P("rows", None),
            P("rows", None),
            P("rows", None),
            P(None, "rows"),
            P(None, "rows"),
        ),
        out_specs=(P(None, "rows"), P()),
        check_vma=False,
    )
```

profile of v0, /device:TPU:0, one launch (start us, length us, event | category | flops | bytes accessed | tf_op | source)
XLA Modules:
  0.0 203.4 jit_solution(11959453189386857067)
XLA Ops:
  0.7 0.9 fusion.37
  1.6 2.5 %collective-permute-start = (f32[32,256]{1,0:T(8,128)S(1)}, f32[32,256]{1,0:T(8,128)S(1)}, u32[]{:S(2)}, u32[]{:S(2)}) collective-permute-start(f32[32,256]{1,0:T(8,128)S(1)} %get-tuple-element.21), channel_id=1, source_target_pairs={{0,1},{1,2},{2,3},{3,4},{4,5},{5,6},{6,7},{7,8},{8,9},{9,10},{10,1... | collective-permute-start | bytes 98312 | tf_op jit(solution)/shard_map/ppermute | solution.py:17
  4.1 1.3 collective-permute-start.1
  5.4 3.9 %collective-permute-done.1 = f32[32,256]{1,0:T(8,128)S(1)} collective-permute-done((f32[32,256]{1,0:T(8,128)S(1)}, f32[32,256]{1,0:T(8,128)S(1)}, u32[]{:S(2)}, u32[]{:S(2)}) %collective-permute-start.1) | collective-permute-done | bytes 32800 | tf_op jit(solution)/shard_map/ppermute | solution.py:20
  9.3 1.6 pad_maximum_fusion
  10.9 1.0 reshape.31
  12.0 0.7 fusion.15
  12.7 0.4 copy-done.2
  13.1 0.7 convolution_add_fusion.5
  13.9 0.7 fusion.4
  14.6 0.5 fusion.23
  15.1 1.3 collective-permute-start.2
  16.5 5.2 %collective-permute-start.5 = (f32[256,256]{1,0:T(8,128)S(1)}, f32[256,256]{1,0:T(8,128)S(1)}, u32[]{:S(2)}, u32[]{:S(2)}) collective-permute-start(f32[256,256]{1,0:T(8,128)S(1)} %convert_negate_fusion), channel_id=1, source_target_pairs={{0,1},{1,2},{2,3},{3,4},{4,5},{5,6},{6,7},{7,8},{8,9},{9,10},{10,1... | collective-permute-start | bytes 786440 | tf_op jit(solution)/shard_map/ppermute | solution.py:28
  21.9 3.6 %collective-permute-start.3 = (f32[32,256]{1,0:T(8,128)S(1)}, f32[32,256]{1,0:T(8,128)S(1)}, u32[]{:S(2)}, u32[]{:S(2)}) collective-permute-start(f32[32,256]{1,0:T(8,128)S(1)} %convolution_subtract_fusion.7), channel_id=1, source_target_pairs={{0,1},{1,2},{2,3},{3,4},{4,5},{5,6},{6,7},{7,8},{8,9},{9,10},{10,1... | collective-permute-start | bytes 98312 | tf_op jit(solution)/shard_map/ppermute | solution.py:28
  25.5 0.8 collective-permute-done.3
  26.4 2.9 %collective-permute-start.4 = (f32[32,256]{1,0:T(8,128)S(1)}, f32[32,256]{1,0:T(8,128)S(1)}, u32[]{:S(2)}, u32[]{:S(2)}) collective-permute-start(f32[32,256]{1,0:T(8,128)S(1)} %collective-permute-done.3), channel_id=1, source_target_pairs={{0,1},{1,2},{2,3},{3,4},{4,5},{5,6},{6,7},{7,8},{8,9},{9,10},{10,1... | collective-permute-start | bytes 98312 | tf_op jit(solution)/shard_map/ppermute | solution.py:28
  29.3 4.4 %collective-permute-start.7 = (f32[256,256]{1,0:T(8,128)S(1)}, f32[256,256]{1,0:T(8,128)S(1)}, u32[]{:S(2)}, u32[]{:S(2)}) collective-permute-start(f32[256,256]{1,0:T(8,128)S(1)} %collective-permute-done.5), channel_id=1, source_target_pairs={{0,1},{1,2},{2,3},{3,4},{4,5},{5,6},{6,7},{7,8},{8,9},{9,10},{10,1... | collective-permute-start | bytes 786440 | tf_op jit(solution)/shard_map/ppermute | solution.py:28
  34.0 5.7 %collective-permute-start.6 = (f32[32,256]{1,0:T(8,128)S(1)}, f32[32,256]{1,0:T(8,128)S(1)}, u32[]{:S(2)}, u32[]{:S(2)}) collective-permute-start(f32[32,256]{1,0:T(8,128)S(1)} %convolution_add_fusion.15), channel_id=1, source_target_pairs={{0,2},{1,3},{2,4},{3,5},{4,6},{5,7},{6,8},{7,9},{8,10},{9,11},{10,... | collective-permute-start | bytes 98312 | tf_op jit(solution)/shard_map/ppermute | solution.py:28
  39.7 0.4 fusion.38
  40.1 4.1 %collective-permute-start.9 = (f32[256,256]{1,0:T(8,128)S(1)}, f32[256,256]{1,0:T(8,128)S(1)}, u32[]{:S(2)}, u32[]{:S(2)}) collective-permute-start(f32[256,256]{1,0:T(8,128)S(1)} %fusion.38), channel_id=1, source_target_pairs={{0,2},{1,3},{2,4},{3,5},{4,6},{5,7},{6,8},{7,9},{8,10},{9,11},{10,... | collective-permute-start | bytes 786440 | tf_op jit(solution)/shard_map/ppermute | solution.py:28
  44.5 7.1 %collective-permute-start.8 = (f32[32,256]{1,0:T(8,128)S(1)}, f32[32,256]{1,0:T(8,128)S(1)}, u32[]{:S(2)}, u32[]{:S(2)}) collective-permute-start(f32[32,256]{1,0:T(8,128)S(1)} %convolution_add_fusion.14), channel_id=1, source_target_pairs={{0,4},{1,5},{2,6},{3,7},{4,8},{5,9},{6,10},{7,11},{8,12},{9,13},{1... | collective-permute-start | bytes 98312 | tf_op jit(solution)/shard_map/ppermute | solution.py:28
  52.0 5.5 %collective-permute-start.11 = (f32[256,256]{1,0:T(8,128)S(1)}, f32[256,256]{1,0:T(8,128)S(1)}, u32[]{:S(2)}, u32[]{:S(2)}) collective-permute-start(f32[256,256]{1,0:T(8,128)S(1)} %fusion.39), channel_id=1, source_target_pairs={{0,4},{1,5},{2,6},{3,7},{4,8},{5,9},{6,10},{7,11},{8,12},{9,13},{1... | collective-permute-start | bytes 786440 | tf_op jit(solution)/shard_map/ppermute | solution.py:28
  57.8 4.1 %collective-permute-start.10 = (f32[32,256]{1,0:T(8,128)S(1)}, f32[32,256]{1,0:T(8,128)S(1)}, u32[]{:S(2)}, u32[]{:S(2)}) collective-permute-start(f32[32,256]{1,0:T(8,128)S(1)} %convolution_add_fusion.13), channel_id=1, source_target_pairs={{0,8},{1,9},{2,10},{3,11},{4,12},{5,13},{6,14},{7,15},{8,16},{9,17... | collective-permute-start | bytes 98312 | tf_op jit(solution)/shard_map/ppermute | solution.py:28
  62.4 6.9 %collective-permute-start.13 = (f32[256,256]{1,0:T(8,128)S(1)}, f32[256,256]{1,0:T(8,128)S(1)}, u32[]{:S(2)}, u32[]{:S(2)}) collective-permute-start(f32[256,256]{1,0:T(8,128)S(1)} %fusion.40), channel_id=1, source_target_pairs={{0,8},{1,9},{2,10},{3,11},{4,12},{5,13},{6,14},{7,15},{8,16},{9,17... | collective-permute-start | bytes 786440 | tf_op jit(solution)/shard_map/ppermute | solution.py:28
  69.5 4.4 %collective-permute-start.12 = (f32[32,256]{1,0:T(8,128)S(1)}, f32[32,256]{1,0:T(8,128)S(1)}, u32[]{:S(2)}, u32[]{:S(2)}) collective-permute-start(f32[32,256]{1,0:T(8,128)S(1)} %convolution_add_fusion.12), channel_id=1, source_target_pairs={{0,16},{1,17},{2,18},{3,19},{4,20},{5,21},{6,22},{7,23},{8,24},{9,... | collective-permute-start | bytes 98312 | tf_op jit(solution)/shard_map/ppermute | solution.py:28
  74.3 1.2 collective-permute-done.12
  76.0 1.3 collective-permute-start.14
  77.3 1.8 collective-permute-done.14
  79.5 2.1 %collective-permute-start.15 = (f32[32,256]{1,0:T(8,128)S(1)}, f32[32,256]{1,0:T(8,128)S(1)}, u32[]{:S(2)}, u32[]{:S(2)}) collective-permute-start(f32[32,256]{1,0:T(8,128)S(1)} %get-tuple-element.19), channel_id=1, source_target_pairs={{0,1},{1,2},{2,3},{3,4},{4,5},{5,6},{6,7},{7,8},{8,9},{9,10},{10,1... | collective-permute-start | bytes 98312 | tf_op jit(solution)/shard_map/ppermute | solution.py:17
  81.6 1.3 collective-permute-start.16
  82.9 1.8 collective-permute-done.16
  84.7 0.7 pad_maximum_fusion.1
  85.4 1.7 reshape.36
  87.1 1.4 fusion.33
  88.4 0.7 fusion.11
  89.2 0.7 convolution_add_fusion.3
  89.9 0.7 fusion.3
  90.7 0.5 fusion.21
  91.2 1.3 collective-permute-start.17
  92.5 3.5 %collective-permute-done.17 = f32[32,256]{1,0:T(8,128)S(1)} collective-permute-done((f32[32,256]{1,0:T(8,128)S(1)}, f32[32,256]{1,0:T(8,128)S(1)}, u32[]{:S(2)}, u32[]{:S(2)}) %collective-permute-start.17) | collective-permute-done | bytes 32800 | tf_op jit(solution)/shard_map/ppermute | solution.py:28
  96.2 4.5 %collective-permute-start.18 = (f32[32,256]{1,0:T(8,128)S(1)}, f32[32,256]{1,0:T(8,128)S(1)}, u32[]{:S(2)}, u32[]{:S(2)}) collective-permute-start(f32[32,256]{1,0:T(8,128)S(1)} %convolution_subtract_fusion.5), channel_id=1, source_target_pairs={{0,1},{1,2},{2,3},{3,4},{4,5},{5,6},{6,7},{7,8},{8,9},{9,10},{10,1... | collective-permute-start | bytes 98312 | tf_op jit(solution)/shard_map/ppermute | solution.py:28
  100.7 0.8 collective-permute-done.18
  101.5 2.2 %collective-permute-start.19 = (f32[32,256]{1,0:T(8,128)S(1)}, f32[32,256]{1,0:T(8,128)S(1)}, u32[]{:S(2)}, u32[]{:S(2)}) collective-permute-start(f32[32,256]{1,0:T(8,128)S(1)} %collective-permute-done.18), channel_id=1, source_target_pairs={{0,1},{1,2},{2,3},{3,4},{4,5},{5,6},{6,7},{7,8},{8,9},{9,10},{10,1... | collective-permute-start | bytes 98312 | tf_op jit(solution)/shard_map/ppermute | solution.py:28
  103.8 0.8 collective-permute-done.19
  104.9 6.4 %collective-permute-start.20 = (f32[32,256]{1,0:T(8,128)S(1)}, f32[32,256]{1,0:T(8,128)S(1)}, u32[]{:S(2)}, u32[]{:S(2)}) collective-permute-start(f32[32,256]{1,0:T(8,128)S(1)} %convolution_add_fusion.10), channel_id=1, source_target_pairs={{0,2},{1,3},{2,4},{3,5},{4,6},{5,7},{6,8},{7,9},{8,10},{9,11},{10,... | collective-permute-start | bytes 98312 | tf_op jit(solution)/shard_map/ppermute | solution.py:28
  111.3 1.7 collective-permute-done.20
  113.3 7.5 %collective-permute-start.21 = (f32[32,256]{1,0:T(8,128)S(1)}, f32[32,256]{1,0:T(8,128)S(1)}, u32[]{:S(2)}, u32[]{:S(2)}) collective-permute-start(f32[32,256]{1,0:T(8,128)S(1)} %convolution_add_fusion.9), channel_id=1, source_target_pairs={{0,4},{1,5},{2,6},{3,7},{4,8},{5,9},{6,10},{7,11},{8,12},{9,13},{1... | collective-permute-start | bytes 98312 | tf_op jit(solution)/shard_map/ppermute | solution.py:28
  120.8 1.6 collective-permute-done.21
  122.6 11.6 %collective-permute-start.22 = (f32[32,256]{1,0:T(8,128)S(1)}, f32[32,256]{1,0:T(8,128)S(1)}, u32[]{:S(2)}, u32[]{:S(2)}) collective-permute-start(f32[32,256]{1,0:T(8,128)S(1)} %convolution_add_fusion.8), channel_id=1, source_target_pairs={{0,8},{1,9},{2,10},{3,11},{4,12},{5,13},{6,14},{7,15},{8,16},{9,17... | collective-permute-start | bytes 98312 | tf_op jit(solution)/shard_map/ppermute | solution.py:28
  134.3 1.6 collective-permute-done.22
  136.1 6.8 %collective-permute-start.23 = (f32[32,256]{1,0:T(8,128)S(1)}, f32[32,256]{1,0:T(8,128)S(1)}, u32[]{:S(2)}, u32[]{:S(2)}) collective-permute-start(f32[32,256]{1,0:T(8,128)S(1)} %convolution_add_fusion.7), channel_id=1, source_target_pairs={{0,16},{1,17},{2,18},{3,19},{4,20},{5,21},{6,22},{7,23},{8,24},{9,... | collective-permute-start | bytes 98312 | tf_op jit(solution)/shard_map/ppermute | solution.py:28
  142.9 1.6 collective-permute-done.23
  145.0 1.3 collective-permute-start.24
  146.3 1.8 collective-permute-done.24
  148.5 2.1 %collective-permute-start.25 = (f32[32,256]{1,0:T(8,128)S(1)}, f32[32,256]{1,0:T(8,128)S(1)}, u32[]{:S(2)}, u32[]{:S(2)}) collective-permute-start(f32[32,256]{1,0:T(8,128)S(1)} %get-tuple-element.17), channel_id=1, source_target_pairs={{0,1},{1,2},{2,3},{3,4},{4,5},{5,6},{6,7},{7,8},{8,9},{9,10},{10,1... | collective-permute-start | bytes 98312 | tf_op jit(solution)/shard_map/ppermute | solution.py:17
  150.5 1.5 collective-permute-start.26
  152.0 1.6 collective-permute-done.26
  153.6 0.7 pad_maximum_fusion.2
  154.3 1.0 reshape.38
  155.5 0.7 fusion.7
  156.6 0.7 convolution_add_fusion.1
  157.3 0.7 fusion.2
  158.2 44.6 %all-reduce = (f32[1,32]{1,0:T(1,128)S(1)}, f32[1,32]{1,0:T(1,128)S(1)}, f32[1,32]{1,0:T(1,128)S(1)}) all-reduce(f32[1,32]{1,0:T(1,128)S(1)} %bitcast.83, f32[1,32]{1,0:T(1,128)S(1)} %bitcast.82, f32[1,32]{1,0:T(1,128)S(1)} %bitcast.81), channel_id=1, replica_groups=mesh['rows'=32] {'rows'}, use_global_device_ids=true, to_apply=%region_5.0 | all-reduce | flops 96 | bytes 768 | tf_op jit(solution)/shard_map/psum | solution.py:78
  202.8 0.6 fusion.31
  (102 shorter events, 6.1 us)
Async XLA Ops:
  0.6 14.0 %copy-start = (bf16[1024,1024]{1,0:T(8,128)(2,1)S(1)}, bf16[1024,1024]{1,0:T(8,128)(2,1)}, u32[]{:S(2)}) copy-start(bf16[1024,1024]{1,0:T(8,128)(2,1)} %param.13) | copy-start | bytes 6291460
  0.6 11.4 %copy-start.1 = (f32[1024,256]{1,0:T(8,128)S(1)}, f32[1024,256]{1,0:T(8,128)}, u32[]{:S(2)}) copy-start(f32[1024,256]{1,0:T(8,128)} %param.10) | copy-start | bytes 3145732
  1.6 3.8 %collective-permute-start = (f32[32,256]{1,0:T(8,128)S(1)}, f32[32,256]{1,0:T(8,128)S(1)}, u32[]{:S(2)}, u32[]{:S(2)}) collective-permute-start(f32[32,256]{1,0:T(8,128)S(1)} %get-tuple-element.21), channel_id=1, source_target_pairs={{0,1},{1,2},{2,3},{3,4},{4,5},{5,6},{6,7},{7,8},{8,9},{9,10},{10,1... | collective-permute-start | bytes 98312 | tf_op jit(solution)/shard_map/ppermute | solution.py:17
  4.1 5.2 %collective-permute-start.1 = (f32[32,256]{1,0:T(8,128)S(1)}, f32[32,256]{1,0:T(8,128)S(1)}, u32[]{:S(2)}, u32[]{:S(2)}) collective-permute-start(f32[32,256]{1,0:T(8,128)S(1)} %get-tuple-element.22), channel_id=1, source_target_pairs={{1,0},{2,1},{3,2},{4,3},{5,4},{6,5},{7,6},{8,7},{9,8},{10,9},{11,1... | collective-permute-start | bytes 98312 | tf_op jit(solution)/shard_map/ppermute | solution.py:20
  11.9 1.2 copy-start.2
  11.9 1.9 copy-start.5
  12.0 2.6 %copy-start.20 = (f32[32,1024]{1,0:T(8,128)S(1)}, f32[32,1024]{1,0:T(8,128)}, u32[]{:S(2)}) copy-start(f32[32,1024]{1,0:T(8,128)} %param.8) | copy-start | bytes 393220
  13.9 2.6 %copy-start.12 = (bf16[256,1024]{1,0:T(8,128)(2,1)S(1)}, bf16[256,1024]{1,0:T(8,128)(2,1)}, u32[]{:S(2)}) copy-start(bf16[256,1024]{1,0:T(8,128)(2,1)} %param.15) | copy-start | bytes 1572868
  13.9 7.8 %copy-start.14 = (bf16[256,1024]{1,0:T(8,128)(2,1)S(1)}, bf16[256,1024]{1,0:T(8,128)(2,1)}, u32[]{:S(2)}) copy-start(bf16[256,1024]{1,0:T(8,128)(2,1)} %param.14) | copy-start | bytes 1572868
  14.6 25.5 %copy-start.23 = (f32[4,4,8,256]{3,2,0,1:T(8,128)}, f32[4,4,8,256]{3,2,0,1:T(8,128)S(1)}, u32[]{:S(2)}) copy-start(f32[4,4,8,256]{3,2,0,1:T(8,128)S(1)} %copy.37) | copy-start | bytes 393220
  15.1 6.5 %collective-permute-start.2 = (f32[32,256]{1,0:T(8,128)S(1)}, f32[32,256]{1,0:T(8,128)S(1)}, u32[]{:S(2)}, u32[]{:S(2)}) collective-permute-start(f32[32,256]{1,0:T(8,128)S(1)} %slice.91), channel_id=1, source_target_pairs={{1,0},{2,1},{3,2},{4,3},{5,4},{6,5},{7,6},{8,7},{9,8},{10,9},{11,1... | collective-permute-start | bytes 98312 | tf_op jit(solution)/shard_map/ppermute | solution.py:28
  16.5 12.8 %collective-permute-start.5 = (f32[256,256]{1,0:T(8,128)S(1)}, f32[256,256]{1,0:T(8,128)S(1)}, u32[]{:S(2)}, u32[]{:S(2)}) collective-permute-start(f32[256,256]{1,0:T(8,128)S(1)} %convert_negate_fusion), channel_id=1, source_target_pairs={{0,1},{1,2},{2,3},{3,4},{4,5},{5,6},{6,7},{7,8},{8,9},{9,10},{10,1... | collective-permute-start | bytes 786440 | tf_op jit(solution)/shard_map/ppermute | solution.py:28
  21.9 4.5 %collective-permute-start.3 = (f32[32,256]{1,0:T(8,128)S(1)}, f32[32,256]{1,0:T(8,128)S(1)}, u32[]{:S(2)}, u32[]{:S(2)}) collective-permute-start(f32[32,256]{1,0:T(8,128)S(1)} %convolution_subtract_fusion.7), channel_id=1, source_target_pairs={{0,1},{1,2},{2,3},{3,4},{4,5},{5,6},{6,7},{7,8},{8,9},{9,10},{10,1... | collective-permute-start | bytes 98312 | tf_op jit(solution)/shard_map/ppermute | solution.py:28
  26.4 7.4 %collective-permute-start.4 = (f32[32,256]{1,0:T(8,128)S(1)}, f32[32,256]{1,0:T(8,128)S(1)}, u32[]{:S(2)}, u32[]{:S(2)}) collective-permute-start(f32[32,256]{1,0:T(8,128)S(1)} %collective-permute-done.3), channel_id=1, source_target_pairs={{0,1},{1,2},{2,3},{3,4},{4,5},{5,6},{6,7},{7,8},{8,9},{9,10},{10,1... | collective-permute-start | bytes 98312 | tf_op jit(solution)/shard_map/ppermute | solution.py:28
  29.3 22.3 %copy-start.16 = (f32[256,256]{1,0:T(8,128)}, f32[256,256]{1,0:T(8,128)S(1)}, u32[]{:S(2)}) copy-start(f32[256,256]{1,0:T(8,128)S(1)} %collective-permute-done.5) | copy-start | bytes 786436
  29.3 10.4 %collective-permute-start.7 = (f32[256,256]{1,0:T(8,128)S(1)}, f32[256,256]{1,0:T(8,128)S(1)}, u32[]{:S(2)}, u32[]{:S(2)}) collective-permute-start(f32[256,256]{1,0:T(8,128)S(1)} %collective-permute-done.5), channel_id=1, source_target_pairs={{0,1},{1,2},{2,3},{3,4},{4,5},{5,6},{6,7},{7,8},{8,9},{9,10},{10,1... | collective-permute-start | bytes 786440 | tf_op jit(solution)/shard_map/ppermute | solution.py:28
  34.0 10.2 %collective-permute-start.6 = (f32[32,256]{1,0:T(8,128)S(1)}, f32[32,256]{1,0:T(8,128)S(1)}, u32[]{:S(2)}, u32[]{:S(2)}) collective-permute-start(f32[32,256]{1,0:T(8,128)S(1)} %convolution_add_fusion.15), channel_id=1, source_target_pairs={{0,2},{1,3},{2,4},{3,5},{4,6},{5,7},{6,8},{7,9},{8,10},{9,11},{10,... | collective-permute-start | bytes 98312 | tf_op jit(solution)/shard_map/ppermute | solution.py:28
  40.1 11.5 %collective-permute-start.9 = (f32[256,256]{1,0:T(8,128)S(1)}, f32[256,256]{1,0:T(8,128)S(1)}, u32[]{:S(2)}, u32[]{:S(2)}) collective-permute-start(f32[256,256]{1,0:T(8,128)S(1)} %fusion.38), channel_id=1, source_target_pairs={{0,2},{1,3},{2,4},{3,5},{4,6},{5,7},{6,8},{7,9},{8,10},{9,11},{10,... | collective-permute-start | bytes 786440 | tf_op jit(solution)/shard_map/ppermute | solution.py:28
  44.5 34.8 %copy-start.27 = (f32[32,1024]{1,0:T(8,128)S(1)}, f32[32,1024]{1,0:T(8,128)}, u32[]{:S(2)}) copy-start(f32[32,1024]{1,0:T(8,128)} %param.9) | copy-start | bytes 393220
  44.5 13.0 %collective-permute-start.8 = (f32[32,256]{1,0:T(8,128)S(1)}, f32[32,256]{1,0:T(8,128)S(1)}, u32[]{:S(2)}, u32[]{:S(2)}) collective-permute-start(f32[32,256]{1,0:T(8,128)S(1)} %convolution_add_fusion.14), channel_id=1, source_target_pairs={{0,4},{1,5},{2,6},{3,7},{4,8},{5,9},{6,10},{7,11},{8,12},{9,13},{1... | collective-permute-start | bytes 98312 | tf_op jit(solution)/shard_map/ppermute | solution.py:28
  52.0 27.4 %copy-start.8 = (f32[256,256]{1,0:T(8,128)}, f32[256,256]{1,0:T(8,128)S(1)}, u32[]{:S(2)}) copy-start(f32[256,256]{1,0:T(8,128)S(1)} %fusion.39) | copy-start | bytes 786436
  52.0 10.0 %collective-permute-start.11 = (f32[256,256]{1,0:T(8,128)S(1)}, f32[256,256]{1,0:T(8,128)S(1)}, u32[]{:S(2)}, u32[]{:S(2)}) collective-permute-start(f32[256,256]{1,0:T(8,128)S(1)} %fusion.39), channel_id=1, source_target_pairs={{0,4},{1,5},{2,6},{3,7},{4,8},{5,9},{6,10},{7,11},{8,12},{9,13},{1... | collective-permute-start | bytes 786440 | tf_op jit(solution)/shard_map/ppermute | solution.py:28
  57.8 11.5 %collective-permute-start.10 = (f32[32,256]{1,0:T(8,128)S(1)}, f32[32,256]{1,0:T(8,128)S(1)}, u32[]{:S(2)}, u32[]{:S(2)}) collective-permute-start(f32[32,256]{1,0:T(8,128)S(1)} %convolution_add_fusion.13), channel_id=1, source_target_pairs={{0,8},{1,9},{2,10},{3,11},{4,12},{5,13},{6,14},{7,15},{8,16},{9,17... | collective-permute-start | bytes 98312 | tf_op jit(solution)/shard_map/ppermute | solution.py:28
  62.4 17.1 %copy-start.10 = (f32[256,256]{1,0:T(8,128)}, f32[256,256]{1,0:T(8,128)S(1)}, u32[]{:S(2)}) copy-start(f32[256,256]{1,0:T(8,128)S(1)} %fusion.40) | copy-start | bytes 786436
  62.4 11.5 %collective-permute-start.13 = (f32[256,256]{1,0:T(8,128)S(1)}, f32[256,256]{1,0:T(8,128)S(1)}, u32[]{:S(2)}, u32[]{:S(2)}) collective-permute-start(f32[256,256]{1,0:T(8,128)S(1)} %fusion.40), channel_id=1, source_target_pairs={{0,8},{1,9},{2,10},{3,11},{4,12},{5,13},{6,14},{7,15},{8,16},{9,17... | collective-permute-start | bytes 786440 | tf_op jit(solution)/shard_map/ppermute | solution.py:28
  69.5 6.0 %collective-permute-start.12 = (f32[32,256]{1,0:T(8,128)S(1)}, f32[32,256]{1,0:T(8,128)S(1)}, u32[]{:S(2)}, u32[]{:S(2)}) collective-permute-start(f32[32,256]{1,0:T(8,128)S(1)} %convolution_add_fusion.12), channel_id=1, source_target_pairs={{0,16},{1,17},{2,18},{3,19},{4,20},{5,21},{6,22},{7,23},{8,24},{9,... | collective-permute-start | bytes 98312 | tf_op jit(solution)/shard_map/ppermute | solution.py:28
  74.3 5.2 %copy-start.18 = (f32[256,256]{1,0:T(8,128)}, f32[256,256]{1,0:T(8,128)S(1)}, u32[]{:S(2)}) copy-start(f32[256,256]{1,0:T(8,128)S(1)} %fusion.41) | copy-start | bytes 786436
  76.0 3.1 %collective-permute-start.14 = (bf16[32,256]{1,0:T(8,128)(2,1)S(1)}, bf16[32,256]{1,0:T(8,128)(2,1)S(1)}, u32[]{:S(2)}, u32[]{:S(2)}) collective-permute-start(bf16[32,256]{1,0:T(8,128)(2,1)S(1)} %convolution_subtract_fusion.6), channel_id=1, source_target_pairs={{1,0},{2,1},{3,2},{4,3},{5,4},{6,5},{7,6},{8,7},{9,8},{10,9},{11,1... | collective-permute-start | bytes 49160 | tf_op jit(solution)/shard_map/ppermute | solution.py:28
  79.5 3.4 %collective-permute-start.15 = (f32[32,256]{1,0:T(8,128)S(1)}, f32[32,256]{1,0:T(8,128)S(1)}, u32[]{:S(2)}, u32[]{:S(2)}) collective-permute-start(f32[32,256]{1,0:T(8,128)S(1)} %get-tuple-element.19), channel_id=1, source_target_pairs={{0,1},{1,2},{2,3},{3,4},{4,5},{5,6},{6,7},{7,8},{8,9},{9,10},{10,1... | collective-permute-start | bytes 98312 | tf_op jit(solution)/shard_map/ppermute | solution.py:17
  81.6 3.1 %collective-permute-start.16 = (f32[32,256]{1,0:T(8,128)S(1)}, f32[32,256]{1,0:T(8,128)S(1)}, u32[]{:S(2)}, u32[]{:S(2)}) collective-permute-start(f32[32,256]{1,0:T(8,128)S(1)} %get-tuple-element.20), channel_id=1, source_target_pairs={{1,0},{2,1},{3,2},{4,3},{5,4},{6,5},{7,6},{8,7},{9,8},{10,9},{11,1... | collective-permute-start | bytes 98312 | tf_op jit(solution)/shard_map/ppermute | solution.py:20
  87.1 2.1 %copy-start.3 = (f32[1024,256]{1,0:T(8,128)S(1)}, f32[1024,256]{1,0:T(8,128)}, u32[]{:S(2)}) copy-start(f32[1024,256]{1,0:T(8,128)} %param.11) | copy-start | bytes 3145732
  87.1 2.8 %copy-start.6 = (f32[1024,256]{1,0:T(8,128)S(1)}, f32[1024,256]{1,0:T(8,128)}, u32[]{:S(2)}) copy-start(f32[1024,256]{1,0:T(8,128)} %param.12) | copy-start | bytes 3145732
  88.4 2.3 %copy-start.21 = (f32[32,1024]{1,0:T(8,128)S(1)}, f32[32,1024]{1,0:T(8,128)}, u32[]{:S(2)}) copy-start(f32[32,1024]{1,0:T(8,128)} %param.8) | copy-start | bytes 393220
  89.9 6.1 %copy-start.15 = (bf16[256,1024]{1,0:T(8,128)(2,1)S(1)}, bf16[256,1024]{1,0:T(8,128)(2,1)}, u32[]{:S(2)}) copy-start(bf16[256,1024]{1,0:T(8,128)(2,1)} %param.14) | copy-start | bytes 1572868
  89.9 14.7 %copy-start.17 = (f32[256,256]{1,0:T(8,128)S(1)}, f32[256,256]{1,0:T(8,128)}, u32[]{:S(2)}) copy-start(f32[256,256]{1,0:T(8,128)} %copy-done.16) | copy-start | bytes 786436
  90.6 31.7 %copy-start.9 = (f32[256,256]{1,0:T(8,128)S(1)}, f32[256,256]{1,0:T(8,128)}, u32[]{:S(2)}) copy-start(f32[256,256]{1,0:T(8,128)} %copy-done.8) | copy-start | bytes 786436
  90.6 45.2 %copy-start.11 = (f32[256,256]{1,0:T(8,128)S(1)}, f32[256,256]{1,0:T(8,128)}, u32[]{:S(2)}) copy-start(f32[256,256]{1,0:T(8,128)} %copy-done.10) | copy-start | bytes 786436
  90.7 45.4 %copy-start.25 = (f32[4,4,8,256]{3,2,0,1:T(8,128)}, f32[4,4,8,256]{3,2,0,1:T(8,128)S(1)}, u32[]{:S(2)}) copy-start(f32[4,4,8,256]{3,2,0,1:T(8,128)S(1)} %copy.38) | copy-start | bytes 393220
  90.7 53.8 %copy-start.19 = (f32[256,256]{1,0:T(8,128)S(1)}, f32[256,256]{1,0:T(8,128)}, u32[]{:S(2)}) copy-start(f32[256,256]{1,0:T(8,128)} %copy-done.18) | copy-start | bytes 786436
  90.7 54.0 %copy-start.13 = (bf16[256,1024]{1,0:T(8,128)(2,1)S(1)}, bf16[256,1024]{1,0:T(8,128)(2,1)}, u32[]{:S(2)}) copy-start(bf16[256,1024]{1,0:T(8,128)(2,1)} %param.15) | copy-start | bytes 1572868
  91.2 4.8 %collective-permute-start.17 = (f32[32,256]{1,0:T(8,128)S(1)}, f32[32,256]{1,0:T(8,128)S(1)}, u32[]{:S(2)}, u32[]{:S(2)}) collective-permute-start(f32[32,256]{1,0:T(8,128)S(1)} %slice.98), channel_id=1, source_target_pairs={{1,0},{2,1},{3,2},{4,3},{5,4},{6,5},{7,6},{8,7},{9,8},{10,9},{11,1... | collective-permute-start | bytes 98312 | tf_op jit(solution)/shard_map/ppermute | solution.py:28
  96.2 5.4 %collective-permute-start.18 = (f32[32,256]{1,0:T(8,128)S(1)}, f32[32,256]{1,0:T(8,128)S(1)}, u32[]{:S(2)}, u32[]{:S(2)}) collective-permute-start(f32[32,256]{1,0:T(8,128)S(1)} %convolution_subtract_fusion.5), channel_id=1, source_target_pairs={{0,1},{1,2},{2,3},{3,4},{4,5},{5,6},{6,7},{7,8},{8,9},{9,10},{10,1... | collective-permute-start | bytes 98312 | tf_op jit(solution)/shard_map/ppermute | solution.py:28
  101.5 3.1 %collective-permute-start.19 = (f32[32,256]{1,0:T(8,128)S(1)}, f32[32,256]{1,0:T(8,128)S(1)}, u32[]{:S(2)}, u32[]{:S(2)}) collective-permute-start(f32[32,256]{1,0:T(8,128)S(1)} %collective-permute-done.18), channel_id=1, source_target_pairs={{0,1},{1,2},{2,3},{3,4},{4,5},{5,6},{6,7},{7,8},{8,9},{9,10},{10,1... | collective-permute-start | bytes 98312 | tf_op jit(solution)/shard_map/ppermute | solution.py:28
  104.9 8.1 %collective-permute-start.20 = (f32[32,256]{1,0:T(8,128)S(1)}, f32[32,256]{1,0:T(8,128)S(1)}, u32[]{:S(2)}, u32[]{:S(2)}) collective-permute-start(f32[32,256]{1,0:T(8,128)S(1)} %convolution_add_fusion.10), channel_id=1, source_target_pairs={{0,2},{1,3},{2,4},{3,5},{4,6},{5,7},{6,8},{7,9},{8,10},{9,11},{10,... | collective-permute-start | bytes 98312 | tf_op jit(solution)/shard_map/ppermute | solution.py:28
  113.3 9.1 %collective-permute-start.21 = (f32[32,256]{1,0:T(8,128)S(1)}, f32[32,256]{1,0:T(8,128)S(1)}, u32[]{:S(2)}, u32[]{:S(2)}) collective-permute-start(f32[32,256]{1,0:T(8,128)S(1)} %convolution_add_fusion.9), channel_id=1, source_target_pairs={{0,4},{1,5},{2,6},{3,7},{4,8},{5,9},{6,10},{7,11},{8,12},{9,13},{1... | collective-permute-start | bytes 98312 | tf_op jit(solution)/shard_map/ppermute | solution.py:28
  122.6 13.2 %collective-permute-start.22 = (f32[32,256]{1,0:T(8,128)S(1)}, f32[32,256]{1,0:T(8,128)S(1)}, u32[]{:S(2)}, u32[]{:S(2)}) collective-permute-start(f32[32,256]{1,0:T(8,128)S(1)} %convolution_add_fusion.8), channel_id=1, source_target_pairs={{0,8},{1,9},{2,10},{3,11},{4,12},{5,13},{6,14},{7,15},{8,16},{9,17... | collective-permute-start | bytes 98312 | tf_op jit(solution)/shard_map/ppermute | solution.py:28
  136.1 8.4 %collective-permute-start.23 = (f32[32,256]{1,0:T(8,128)S(1)}, f32[32,256]{1,0:T(8,128)S(1)}, u32[]{:S(2)}, u32[]{:S(2)}) collective-permute-start(f32[32,256]{1,0:T(8,128)S(1)} %convolution_add_fusion.7), channel_id=1, source_target_pairs={{0,16},{1,17},{2,18},{3,19},{4,20},{5,21},{6,22},{7,23},{8,24},{9,... | collective-permute-start | bytes 98312 | tf_op jit(solution)/shard_map/ppermute | solution.py:28
  145.0 3.1 %collective-permute-start.24 = (bf16[32,256]{1,0:T(8,128)(2,1)S(1)}, bf16[32,256]{1,0:T(8,128)(2,1)S(1)}, u32[]{:S(2)}, u32[]{:S(2)}) collective-permute-start(bf16[32,256]{1,0:T(8,128)(2,1)S(1)} %convolution_subtract_fusion.4), channel_id=1, source_target_pairs={{1,0},{2,1},{3,2},{4,3},{5,4},{6,5},{7,6},{8,7},{9,8},{10,9},{11,1... | collective-permute-start | bytes 49160 | tf_op jit(solution)/shard_map/ppermute | solution.py:28
  148.4 5.2 %copy-start.28 = (f32[32,1024]{1,0:T(8,128)}, f32[32,1024]{1,0:T(8,128)S(1)}, u32[]{:S(2)}) copy-start(f32[32,1024]{1,0:T(8,128)S(1)} %fusion) | copy-start | bytes 393220
  148.5 3.6 %collective-permute-start.25 = (f32[32,256]{1,0:T(8,128)S(1)}, f32[32,256]{1,0:T(8,128)S(1)}, u32[]{:S(2)}, u32[]{:S(2)}) collective-permute-start(f32[32,256]{1,0:T(8,128)S(1)} %get-tuple-element.17), channel_id=1, source_target_pairs={{0,1},{1,2},{2,3},{3,4},{4,5},{5,6},{6,7},{7,8},{8,9},{9,10},{10,1... | collective-permute-start | bytes 98312 | tf_op jit(solution)/shard_map/ppermute | solution.py:17
  150.5 3.1 %collective-permute-start.26 = (f32[32,256]{1,0:T(8,128)S(1)}, f32[32,256]{1,0:T(8,128)S(1)}, u32[]{:S(2)}, u32[]{:S(2)}) collective-permute-start(f32[32,256]{1,0:T(8,128)S(1)} %get-tuple-element.18), channel_id=1, source_target_pairs={{1,0},{2,1},{3,2},{4,3},{5,4},{6,5},{7,6},{8,7},{9,8},{10,9},{11,1... | collective-permute-start | bytes 98312 | tf_op jit(solution)/shard_map/ppermute | solution.py:20
  155.3 1.2 copy-start.4
  155.3 1.9 copy-start.7
  155.4 2.6 %copy-start.22 = (f32[32,1024]{1,0:T(8,128)S(1)}, f32[32,1024]{1,0:T(8,128)}, u32[]{:S(2)}) copy-start(f32[32,1024]{1,0:T(8,128)} %param.8) | copy-start | bytes 393220
  155.4 2.6 %copy-start.24 = (f32[4,4,8,256]{3,2,0,1:T(8,128)S(1)}, f32[4,4,8,256]{3,2,0,1:T(8,128)}, u32[]{:S(2)}) copy-start(f32[4,4,8,256]{3,2,0,1:T(8,128)} %copy-done.23) | copy-start | bytes 393220
  155.4 2.6 %copy-start.26 = (f32[4,4,8,256]{3,2,0,1:T(8,128)S(1)}, f32[4,4,8,256]{3,2,0,1:T(8,128)}, u32[]{:S(2)}) copy-start(f32[4,4,8,256]{3,2,0,1:T(8,128)} %copy-done.25) | copy-start | bytes 393220
where the time goes:
time: 204 us; the launch traced here: 203 us
  starting transfers between devices  109 us (53%)
  blocking collectives  44.6 us (22%)
  waiting for transfers between devices  24.6 us (12%)
  matrix products  12.8 us (6%)
  local copies, waits for them, and re-layouts  7.06 us (3%)
  other arithmetic  3.77 us (2%)
    ppermute x21, starting transfers between devices, shifted(): return lax.ppermute(block, axis, route)  98.2 us
    psum x1, blocking collectives, record_norm(): records.append(lax.psum(partial_sum, 'rows'))  44.6 us
    ppermute x21, waiting for transfers between devices, shifted(): return lax.ppermute(block, axis, route)  17.3 us
    ppermute x3, waiting for transfers between devices, with_halo(): lax.ppermute(lax.slice_in_dim(block, 0, width, axis=dim), axis, backward)  7.29 us
    ppermute x3, starting transfers between devices, with_halo(): lax.ppermute(lax.slice_in_dim(block, block.shape[dim] - width, None, axis...  6.66 us
  transfers between devices with their start and end apart: 27, of which 15 were waited for; matrix products, arithmetic and copies ran while one was open for 1% of the time, Pallas kernels for 0%

commit v1 on v0

v1 whole, which is shorter than its diff:
```python
import jax
import jax.numpy as jnp
from jax import lax
from jax.experimental import pallas as pl
from jax.experimental.pallas import tpu as pltpu
from jax.sharding import PartitionSpec as P

ITERS = 2
GROUP = 8
SUB = 8
LANES = 128
F32 = jnp.float32
BF16 = jnp.bfloat16
MESH = pl.DeviceIdType.MESH


def rcopy(src, dst, send_sem, recv_sem, target):
    return pltpu.make_async_remote_copy(
        src_ref=src,
        dst_ref=dst,
        send_sem=send_sem,
        recv_sem=recv_sem,
        device_id=(target,),
        device_id_type=MESH,
    )


def stacked_split(v):
    hi = v.astype(BF16).astype(F32)
    return jnp.concatenate([hi, v - hi], axis=0).astype(BF16)


def dot(a, b):
    return jnp.dot(a, b, preferred_element_type=F32)


def fold(o):
    half = o.shape[0] // 2
    return o[:half] + o[half:]


def mm2(v, w):
    return fold(dot(stacked_split(v), w))


def make_kernel(n, rhs, cols, band):
    blocks = cols // band
    groups = n // GROUP
    rowblocks = rhs // SUB
    order = float(cols * n)
    tail = cols - band

    def kernel(
        b_hbm, x_hbm, d_hbm, lo_hbm, up_hbm, z_hbm, us_hbm, ls_hbm,
        out_ref, norm_ref,
        b, x, a_f32, z, us, ls, a_hi, a_lo, lg, w_hi, w_lo, uprev, lnext,
        halo_l, halo_r, loc, ntop, msg, inbuf, plbuf, bin_, bout, pout, prevbuf,
        nstack, nrow, nbuf,
        in_sem, l_send, l_recv, nb_send, nb_recv, halo_send, halo_recv,
        nt_send, nt_recv, a_send, a_recv, b_send, b_recv, p_send, p_recv,
        n_send, n_recv,
    ):
        me = lax.axis_index("rows")
        j = lax.rem(me, GROUP)
        g = me // GROUP
        base = me - j
        d = lax.rem(j, rowblocks)
        h = j // rowblocks
        partner = base + j + 1 - 2 * lax.rem(j, 2)
        left = lax.max(me - 1, 0)
        right = lax.min(me + 1, n - 1)
        has_left = me > 0
        has_right = me < n - 1

        loads = [
            pltpu.make_async_copy(x_hbm, x, in_sem.at[0]),
            pltpu.make_async_copy(ls_hbm.at[:, pl.ds(tail, band)], lg.at[j], in_sem.at[1]),
            pltpu.make_async_copy(us_hbm, us, in_sem.at[2]),
            pltpu.make_async_copy(ls_hbm, ls, in_sem.at[3]),
            pltpu.make_async_copy(d_hbm, a_f32.at[1], in_sem.at[4]),
            pltpu.make_async_copy(lo_hbm, a_f32.at[0], in_sem.at[5]),
            pltpu.make_async_copy(up_hbm, a_f32.at[2], in_sem.at[6]),
            pltpu.make_async_copy(b_hbm, b, in_sem.at[7]),
            pltpu.make_async_copy(z_hbm, z, in_sem.at[8]),
        ]
        for c in loads:
            c.start()

        barrier = pltpu.get_barrier_semaphore()

        @pl.loop(1, n)
        def _(k):
            pl.semaphore_signal(
                barrier, inc=1, device_id=(lax.rem(me + k, n),), device_id_type=MESH
            )

        @pl.when(me == 0)
        def _():
            halo_l[...] = jnp.zeros_like(halo_l)
            uprev[...] = jnp.zeros_like(uprev)

        @pl.when(me == n - 1)
        def _():
            halo_r[...] = jnp.zeros_like(halo_r)
            lnext[...] = jnp.zeros_like(lnext)
            ntop[...] = jnp.zeros_like(ntop)

        @pl.when(g == 0)
        def _():
            bin_[...] = jnp.zeros_like(bin_)

        nstack[...] = jnp.zeros_like(nstack)

        def halo_copies(it):
            to_right = rcopy(x.at[:, pl.ds(tail, band)], halo_l.at[it],
                             halo_send.at[it, 0], halo_recv.at[it, 0], right)
            to_left = rcopy(x.at[:, pl.ds(0, band)], halo_r.at[it],
                            halo_send.at[it, 1], halo_recv.at[it, 1], left)
            return to_right, to_left

        def halo_start(it):
            to_right, to_left = halo_copies(it)
            pl.when(has_right)(to_right.start)
            pl.when(has_left)(to_left.start)

        def halo_wait_recv(it):
            to_right, to_left = halo_copies(it)
            pl.when(has_left)(to_right.wait_recv)
            pl.when(has_right)(to_left.wait_recv)

        def halo_wait_send(it):
            to_right, to_left = halo_copies(it)
            pl.when(has_right)(to_right.wait_send)
            pl.when(has_left)(to_left.wait_send)

        loads[0].wait()
        loads[1].wait()
        pl.semaphore_wait(barrier, n - 1)
        halo_start(0)

        l_copies = [rcopy(lg.at[j], lg.at[j], l_send.at[0], l_recv.at[j], partner)]
        for k in range(1, GROUP // 2):
            l_copies.append(
                rcopy(lg.at[j], lg.at[j], l_send.at[k], l_recv.at[j],
                      base + lax.rem(j + 2 * k, GROUP))
            )
        for c in l_copies:
            c.start()
        loads[2].wait()
        loads[3].wait()
        u_copy = rcopy(us.at[:, pl.ds(tail, band)], uprev, nb_send.at[0], nb_recv.at[0], right)
        t_copy = rcopy(ls.at[:, pl.ds(0, band)], lnext, nb_send.at[1], nb_recv.at[1], left)
        pl.when(has_right)(u_copy.start)
        pl.when(has_left)(t_copy.start)

        for part, load in ((1, 4), (0, 5), (2, 6)):
            loads[load].wait()

            @pl.loop(0, blocks)
            def _(k):
                rows = pl.ds(pl.multiple_of(k * band, band), band)
                v = a_f32[part, rows, :]
                hi = v.astype(BF16)
                a_hi[part, k] = hi
                a_lo[part, k] = (v - hi.astype(F32)).astype(BF16)

        loads[7].wait()
        loads[8].wait()

        def residual(it):
            sp = [stacked_split(x[:, k * band:(k + 1) * band]) for k in range(blocks)]

            def term(s, part, k):
                return fold(dot(s, a_hi[part, k])) + dot(s[:rhs], a_lo[part, k])

            acc = []
            for k in range(blocks):
                t = b[:, k * band:(k + 1) * band] - term(sp[k], 1, k)
                if k > 0:
                    t = t - term(sp[k - 1], 0, k)
                if k < blocks - 1:
                    t = t - term(sp[k + 1], 2, k)
                acc.append(t)
            halo_wait_recv(it)
            acc[0] = acc[0] - term(stacked_split(halo_l[it]), 0, 0)
            acc[-1] = acc[-1] - term(stacked_split(halo_r[it]), 2, blocks - 1)
            sq = None
            for t in acc:
                for c in range(band // LANES):
                    v = t[:, c * LANES:(c + 1) * LANES]
                    sq = v * v if sq is None else sq + v * v
            nstack[it * rhs:(it + 1) * rhs, :] = sq
            return acc

        for it in range(ITERS):
            acc = residual(it)
            rounded = jnp.concatenate([t.astype(BF16) for t in acc], axis=1)
            top_own = dot(rounded, z[:, 0:band])
            loc[:, 0:band] = top_own
            nt_copy = rcopy(loc.at[:, pl.ds(0, band)], ntop.at[it],
                            nt_send.at[it], nt_recv.at[it], left)
            pl.when(has_left)(nt_copy.start)
            bot_own = dot(rounded, z[:, tail:])
            if it == 0:
                pl.when(has_left)(u_copy.wait_recv)
            tu = mm2(top_own, uprev[...])
            for r in range(rowblocks):
                msg[it, r, 0] = bot_own[r * SUB:(r + 1) * SUB]
                msg[it, r, 1] = tu[r * SUB:(r + 1) * SUB]
            a_copies = []
            for k in range(1, GROUP):
                t = lax.rem(j + k, GROUP)
                c = rcopy(msg.at[it, lax.rem(t, rowblocks)], inbuf.at[it, j],
                          a_send.at[it, k], a_recv.at[it, j], base + t)
                c.start()
                a_copies.append(c)
            inbuf[it, j] = msg[it, d]
            loc[:, tail:] = bot_own
            for k in range(1, blocks - 1):
                loc[:, k * band:(k + 1) * band] = dot(rounded, z[:, k * band:(k + 1) * band])

            if it == 0:
                for k in range(1, GROUP // 2):
                    owner = lax.rem(j + 2 * k, GROUP)
                    c = rcopy(lg.at[owner], lg.at[owner], l_send.at[GROUP // 2 - 1 + k],
                              l_recv.at[owner], partner)
                    c.wait_recv()
                    c.start()
                    l_copies.append(c)
                for k in range(GROUP // 2):
                    owner = lax.rem(j + 1 - 2 * lax.rem(j, 2) + 2 * k + GROUP, GROUP)
                    rcopy(lg.at[owner], lg.at[owner], l_send.at[0],
                          l_recv.at[owner], partner).wait_recv()
            for k in range(1, GROUP):
                t = lax.rem(j + k, GROUP)
                rcopy(msg.at[it, 0], inbuf.at[it, t], a_send.at[it, k],
                      a_recv.at[it, t], base + t).wait_recv()

            carry = jnp.where(g > 0, -inbuf[it, 0, 1], 0.0)
            plbuf[it, 0] = carry
            for q in range(GROUP):
                carry = inbuf[it, q, 0] - mm2(carry, lg[q])
                if q < GROUP - 1:
                    carry = carry - inbuf[it, q + 1, 1]
                    plbuf[it, q + 1] = carry
            group_end = carry

            bout[it] = group_end
            b_copy = rcopy(bout.at[it], bin_.at[it], b_send.at[it], b_recv.at[it],
                           lax.rem(me + GROUP, n))
            if groups > 1:
                pl.when(g == 0)(b_copy.start)

            if it == 0:
                row = lax.broadcasted_iota(jnp.int32, (band, band), 0)
                col = lax.broadcasted_iota(jnp.int32, (band, band), 1)
                w_hi[0] = jnp.where(row == col, 1.0, 0.0).astype(BF16)
                w_lo[0] = jnp.zeros((band, band), BF16)

                @pl.loop(0, GROUP)
                def _(q):
                    v = -(dot(w_hi[q], lg[q]) + dot(w_lo[q], lg[q]))
                    hi = v.astype(BF16)
                    w_hi[q + 1] = hi
                    w_lo[q + 1] = (v - hi.astype(F32)).astype(BF16)

            if groups > 1:

                @pl.when(g > 0)
                def _():
                    b_copy.wait_recv()

                    @pl.when(g < groups - 1)
                    def _():
                        s = stacked_split(bin_[it])
                        bout[it] = bout[it] + fold(dot(s, w_hi[GROUP])) + fold(dot(s, w_lo[GROUP]))
                        b_copy.start()

            s = stacked_split(bin_[it])
            for i in range(rowblocks):
                q = h * rowblocks + i
                pout[it, i] = plbuf[it, q] + fold(dot(s, w_hi[q])) + fold(dot(s, w_lo[q]))
            p_copies = []
            for k in range(1, rowblocks):
                i = lax.rem(d + k, rowblocks)
                c = rcopy(pout.at[it, i], prevbuf.at[it, d], p_send.at[it, k],
                          p_recv.at[it, d], base + h * rowblocks + i)
                c.start()
                p_copies.append(c)
            prevbuf[it, d] = pout[it, d]

            pl.when(has_right)(nt_copy.wait_recv)
            if it == 0:
                pl.when(has_right)(t_copy.wait_recv)
            next_top = ntop[it]
            offset = loc[:, tail:] - mm2(next_top, us[:, tail:])
            for k in range(1, rowblocks):
                i = lax.rem(d + k, rowblocks)
                rcopy(pout.at[it, i], prevbuf.at[it, i], p_send.at[it, k],
                      p_recv.at[it, i], base + h * rowblocks + i).wait_recv()
            previous = prevbuf[it].reshape(rhs, band)
            bottom = offset - mm2(previous, ls[:, tail:])
            top = next_top - mm2(bottom, lnext[...])
            top = jnp.where(has_right, top, 0.0).astype(BF16)
            prev16 = previous.astype(BF16)
            halo_wait_send(it)

            def update(k):
                c = slice(k * band, (k + 1) * band)
                x[:, c] = x[:, c] + (loc[:, c] - dot(top, us[:, c]) - dot(prev16, ls[:, c]))

            update(0)
            update(blocks - 1)
            halo_start(it + 1)
            for k in range(1, blocks - 1):
                update(k)
            pl.when(has_left)(nt_copy.wait_send)
            for c in a_copies:
                c.wait_send()
            for c in p_copies:
                c.wait_send()
            if groups > 1:
                pl.when(g < groups - 1)(b_copy.wait_send)
            if it == 0:
                for c in l_copies:
                    c.wait_send()
                pl.when(has_right)(u_copy.wait_send)
                pl.when(has_left)(t_copy.wait_send)

        out_ref[...] = x[...]
        residual(ITERS)
        partial = jnp.sum(nstack[...].T, axis=0, keepdims=True)
        nrow[...] = partial
        nbuf[me] = partial

        def norm_copy(k):
            return rcopy(nrow, nbuf.at[me], n_send.at[k], n_recv.at[me], lax.rem(me + k, n))

        @pl.loop(1, n)
        def _(k):
            norm_copy(k).start()

        halo_wait_send(ITERS)

        @pl.loop(1, n)
        def _(k):
            t = lax.rem(me + k, n)
            rcopy(nrow, nbuf.at[t], n_send.at[k], n_recv.at[t], t).wait_recv()

        total = jnp.sqrt(jnp.sum(nbuf[...], axis=0) / order)
        for i in range(ITERS + 1):
            norm_ref[i:i + 1, :] = total[:, i * rhs:(i + 1) * rhs]

        @pl.loop(1, n)
        def _(k):
            norm_copy(k).wait_send()

    return kernel


def body(b, x, dg, lo, up, z, us, ls):
    n = lax.axis_size("rows")
    rhs, cols = b.shape
    band = dg.shape[1]
    blocks = cols // band
    rb = rhs // SUB
    dma = pltpu.SemaphoreType.DMA
    vm = pltpu.VMEM
    scratch = [
        vm((rhs, cols), F32), vm((rhs, cols), F32), vm((3, cols, band), F32),
        vm(z.shape, BF16), vm(us.shape, BF16), vm(ls.shape, BF16),
        vm((3, blocks, band, band), BF16), vm((3, blocks, band, band), BF16),
        vm((GROUP, band, band), BF16),
        vm((GROUP + 1, band, band), BF16), vm((GROUP + 1, band, band), BF16),
        vm((band, band), BF16), vm((band, band), BF16),
        vm((ITERS + 1, rhs, band), F32), vm((ITERS + 1, rhs, band), F32),
        vm((rhs, cols), F32), vm((ITERS, rhs, band), F32),
        vm((ITERS, rb, 2, SUB, band), F32), vm((ITERS, GROUP, 2, SUB, band), F32),
        vm((ITERS, GROUP, SUB, band), F32),
        vm((ITERS, SUB, band), F32), vm((ITERS, SUB, band), F32),
        vm((ITERS, rb, SUB, band), F32), vm((ITERS, rb, SUB, band), F32),
        vm((LANES, LANES), F32), vm((1, LANES), F32), vm((n, 1, LANES), F32),
        dma((9,)), dma((GROUP,)), dma((GROUP,)), dma((2,)), dma((2,)),
        dma((ITERS + 1, 2)), dma((ITERS + 1, 2)),
        dma((ITERS,)), dma((ITERS,)), dma((ITERS, GROUP)), dma((ITERS, GROUP)),
        dma((ITERS,)), dma((ITERS,)), dma((ITERS, rb)), dma((ITERS, rb)),
        dma((n,)), dma((n,)),
    ]
    return pl.pallas_call(
        make_kernel(n, rhs, cols, band),
        out_shape=(
            jax.ShapeDtypeStruct((rhs, cols), F32),
            jax.ShapeDtypeStruct((ITERS + 1, rhs), F32),
        ),
        in_specs=[pl.BlockSpec(memory_space=pl.ANY)] * 8,
        out_specs=(pl.BlockSpec(memory_space=pltpu.VMEM),) * 2,
        scratch_shapes=scratch,
        compiler_params=pltpu.CompilerParams(
            collective_id=0, has_side_effects=True, vmem_limit_bytes=48 * 1024 * 1024
        ),
    )(b, x, dg, lo, up, z, us, ls)


def solution(mesh):
    return jax.shard_map(
        body,
        mesh=mesh,
        in_specs=(
            P(None, "rows"),
            P(None, "rows"),
            P("rows", None),
            P("rows", None),
            P("rows", None),
            P("rows", None),
            P(None, "rows"),
            P(None, "rows"),
        ),
        out_specs=(P(None, "rows"), P()),
        check_vma=False,
    )
```

time: 204 us -> 68.4 us (0.34)
  starting transfers between devices: 109 us -> 0 us
  Pallas kernels: 0 us -> 58.6 us
  blocking collectives: 44.6 us -> 0 us
  waiting for transfers between devices: 24.6 us -> 0 us
  matrix products: 12.8 us -> 0 us
  other arithmetic: 3.77 us -> 0 us
    ppermute x27 -> x0, starting transfers between devices: 109 us -> none  [the longest x21 98.2 us: shifted(): return lax.ppermute(block, axis, route)]
    pallas_call x0 -> x1, Pallas kernels: none -> 58.6 us  [body(): pl.pallas_call(make_kernel(n, rhs, cols, band), out_shape=(jax.ShapeDtype...]
    psum x1 -> x0, blocking collectives: 44.6 us -> none  [record_norm(): records.append(lax.psum(partial_sum, 'rows'))]
    ppermute x27 -> x0, waiting for transfers between devices: 24.6 us -> none  [the longest x21 17.3 us: shifted(): return lax.ppermute(block, axis, route)]
    dot_general x33 -> x0, matrix products: 12.8 us -> none  [the longest x10 2.35 us: body(): jnp.matmul(arrived_sum, level_mats[level_index], precision=maximum_level)]
    unnamed x58 -> x16, local copies, waits for them, and re-layouts: 0.92 us -> 8.79 us
    reshape x6 -> x0, local copies, waits for them, and re-layouts: 3.68 us -> none  [the longest x3 3.65 us: residual_of(): stacked = padded.reshape(padded.shape[0], block_count + 2, band_width)]
    concatenate x3 -> x0, other arithmetic: 2.99 us -> none  [with_halo(): block = jnp.concatenate([low, block, high], axis=dim)]
  transfers between devices with their start and end apart: 27 -> 0, of which waited for: 15 -> 0; matrix products, arithmetic and copies ran while one was open for 1% -> 0% of each run, Pallas kernels for 0% -> 0%
where the time goes in v1:
time: 68.4 us; the launch traced here: 68 us
  Pallas kernels  58.6 us (86%)
  local copies, waits for them, and re-layouts  8.79 us (13%)
    pallas_call x1, Pallas kernels, body(): pl.pallas_call(make_kernel(n, rhs, cols, band), out_shape=(jax.ShapeDtype...  58.6 us
    unnamed x16, local copies, waits for them, and re-layouts  8.79 us

profile of v1, /device:TPU:0, one launch (start us, length us, event | category | flops | bytes accessed | tf_op | source)
XLA Modules:
  0.0 68.0 jit_solution(8157925509264217235)
XLA Ops:
  0.6 0.0 copy-start
  0.6 1.2 %copy-done = f32[1024,256]{1,0:T(8,128)S(1)} copy-done((f32[1024,256]{1,0:T(8,128)S(1)}, f32[1024,256]{1,0:T(8,128)}, u32[]{:S(2)}) %copy-start) | copy-done | bytes 1048600
  1.9 0.0 copy-start.1
  1.9 1.2 %copy-done.1 = f32[1024,256]{1,0:T(8,128)S(1)} copy-done((f32[1024,256]{1,0:T(8,128)S(1)}, f32[1024,256]{1,0:T(8,128)}, u32[]{:S(2)}) %copy-start.1) | copy-done | bytes 1048600
  3.1 0.0 copy-start.2
  3.1 1.2 %copy-done.2 = f32[1024,256]{1,0:T(8,128)S(1)} copy-done((f32[1024,256]{1,0:T(8,128)S(1)}, f32[1024,256]{1,0:T(8,128)}, u32[]{:S(2)}) %copy-start.2) | copy-done | bytes 1048600
  4.3 0.0 copy-start.3
  4.3 1.0 %copy-done.3 = bf16[256,1024]{1,0:T(8,128)(2,1)S(1)} copy-done((bf16[256,1024]{1,0:T(8,128)(2,1)S(1)}, bf16[256,1024]{1,0:T(8,128)(2,1)}, u32[]{:S(2)}) %copy-start.3) | copy-done | bytes 524312
  5.4 0.0 copy-start.4
  5.4 1.0 %copy-done.4 = bf16[256,1024]{1,0:T(8,128)(2,1)S(1)} copy-done((bf16[256,1024]{1,0:T(8,128)(2,1)S(1)}, bf16[256,1024]{1,0:T(8,128)(2,1)}, u32[]{:S(2)}) %copy-start.4) | copy-done | bytes 524312
  6.4 0.0 copy-start.5
  6.4 0.9 %copy-done.5 = f32[32,1024]{1,0:T(8,128)S(1)} copy-done((f32[32,1024]{1,0:T(8,128)S(1)}, f32[32,1024]{1,0:T(8,128)}, u32[]{:S(2)}) %copy-start.5) | copy-done | bytes 131096
  7.3 0.0 copy-start.6
  7.3 0.9 %copy-done.6 = f32[32,1024]{1,0:T(8,128)S(1)} copy-done((f32[32,1024]{1,0:T(8,128)S(1)}, f32[32,1024]{1,0:T(8,128)}, u32[]{:S(2)}) %copy-start.6) | copy-done | bytes 131096
  8.2 58.6 %shard_map.95 = (f32[32,1024]{1,0:T(8,128)S(1)}, f32[3,32]{1,0:T(4,128)S(1)}) custom-call(f32[32,1024]{1,0:T(8,128)S(1)} %copy-done.5, f32[32,1024]{1,0:T(8,128)S(1)} %copy-done.6, f32[1024,256]{1,0:T(8,128)S(1)} %copy-done, f32[1024,256]{1,0:T(8,128)S(1)} %copy-done.1, f32[1024,256]{1,0:T(8,128)S(1)} %copy-done.2, bf16[1024,1024]{1,0:T(8,128)(2,1)} %z_hbm.1, ...), custom_call_target="tpu_custom_call" | custom-call | tf_op jit(solution)/shard_map/pallas_call | solution.py:389
  66.8 0.7 copy.12
  67.4 0.6 copy.13
Async XLA Ops:
  0.6 1.2 %copy-start = (f32[1024,256]{1,0:T(8,128)S(1)}, f32[1024,256]{1,0:T(8,128)}, u32[]{:S(2)}) copy-start(f32[1024,256]{1,0:T(8,128)} %d_hbm.1) | copy-start | bytes 3145732
  1.9 1.2 %copy-start.1 = (f32[1024,256]{1,0:T(8,128)S(1)}, f32[1024,256]{1,0:T(8,128)}, u32[]{:S(2)}) copy-start(f32[1024,256]{1,0:T(8,128)} %lo_hbm.1) | copy-start | bytes 3145732
  3.1 1.2 %copy-start.2 = (f32[1024,256]{1,0:T(8,128)S(1)}, f32[1024,256]{1,0:T(8,128)}, u32[]{:S(2)}) copy-start(f32[1024,256]{1,0:T(8,128)} %up_hbm.1) | copy-start | bytes 3145732
  4.3 1.0 %copy-start.3 = (bf16[256,1024]{1,0:T(8,128)(2,1)S(1)}, bf16[256,1024]{1,0:T(8,128)(2,1)}, u32[]{:S(2)}) copy-start(bf16[256,1024]{1,0:T(8,128)(2,1)} %us_hbm.1) | copy-start | bytes 1572868
  5.4 1.0 %copy-start.4 = (bf16[256,1024]{1,0:T(8,128)(2,1)S(1)}, bf16[256,1024]{1,0:T(8,128)(2,1)}, u32[]{:S(2)}) copy-start(bf16[256,1024]{1,0:T(8,128)(2,1)} %ls_hbm.1) | copy-start | bytes 1572868
  6.4 0.9 %copy-start.5 = (f32[32,1024]{1,0:T(8,128)S(1)}, f32[32,1024]{1,0:T(8,128)}, u32[]{:S(2)}) copy-start(f32[32,1024]{1,0:T(8,128)} %b_hbm.1) | copy-start | bytes 393220
  7.3 0.9 %copy-start.6 = (f32[32,1024]{1,0:T(8,128)S(1)}, f32[32,1024]{1,0:T(8,128)}, u32[]{:S(2)}) copy-start(f32[32,1024]{1,0:T(8,128)} %x_hbm.1) | copy-start | bytes 393220

commit v2 on v1

--- a/solution.py
+++ b/solution.py
@@ -144,14 +144,13 @@
                 rcopy(lg.at[j], lg.at[j], l_send.at[k], l_recv.at[j],
                       base + lax.rem(j + 2 * k, GROUP))
             )
-        for c in l_copies:
-            c.start()
         loads[2].wait()
         loads[3].wait()
         u_copy = rcopy(us.at[:, pl.ds(tail, band)], uprev, nb_send.at[0], nb_recv.at[0], right)
         t_copy = rcopy(ls.at[:, pl.ds(0, band)], lnext, nb_send.at[1], nb_recv.at[1], left)
         pl.when(has_right)(u_copy.start)
-        pl.when(has_left)(t_copy.start)
+        for c in l_copies:
+            c.start()
 
         for part, load in ((1, 4), (0, 5), (2, 6)):
             loads[load].wait()
@@ -227,6 +226,7 @@
                     c.wait_recv()
                     c.start()
                     l_copies.append(c)
+                pl.when(has_left)(t_copy.start)
                 for k in range(GROUP // 2):
                     owner = lax.rem(j + 1 - 2 * lax.rem(j, 2) + 2 * k + GROUP, GROUP)
                     rcopy(lg.at[owner], lg.at[owner], l_send.at[0],
@@ -256,8 +256,10 @@
                 col = lax.broadcasted_iota(jnp.int32, (band, band), 1)
                 w_hi[0] = jnp.where(row == col, 1.0, 0.0).astype(BF16)
                 w_lo[0] = jnp.zeros((band, band), BF16)
-
-                @pl.loop(0, GROUP)
+                w_hi[1] = -lg[0]
+                w_lo[1] = jnp.zeros((band, band), BF16)
+
+                @pl.loop(1, GROUP)
                 def _(q):
                     v = -(dot(w_hi[q], lg[q]) + dot(w_lo[q], lg[q]))
                     hi = v.astype(BF16)
@@ -334,26 +336,22 @@
         nbuf[me] = partial
 
         def norm_copy(k):
-            return rcopy(nrow, nbuf.at[me], n_send.at[k], n_recv.at[me], lax.rem(me + k, n))
-
-        @pl.loop(1, n)
-        def _(k):
-            norm_copy(k).start()
-
+            return rcopy(nrow, nbuf.at[me], n_send.at[0], n_recv.at[0], lax.rem(me + k, n))
+
+        @pl.loop(0, (n - 1) // 2)
+        def _(i):
+            norm_copy(n // 2 + i).start()
+            norm_copy(n // 2 - 1 - i).start()
+
+        norm_copy(n - 1).start()
         halo_wait_send(ITERS)
-
-        @pl.loop(1, n)
-        def _(k):
-            t = lax.rem(me + k, n)
-            rcopy(nrow, nbuf.at[t], n_send.at[k], n_recv.at[t], t).wait_recv()
-
+        everyone = nbuf.at[pl.ds(0, n - 1)]
+        everything = rcopy(everyone, everyone, n_send.at[0], n_recv.at[0], right)
+        everything.wait_recv()
         total = jnp.sqrt(jnp.sum(nbuf[...], axis=0) / order)
         for i in range(ITERS + 1):
             norm_ref[i:i + 1, :] = total[:, i * rhs:(i + 1) * rhs]
-
-        @pl.loop(1, n)
-        def _(k):
-            norm_copy(k).wait_send()
+        everything.wait_send()
 
     return kernel
 
@@ -384,7 +382,7 @@
         dma((ITERS + 1, 2)), dma((ITERS + 1, 2)),
         dma((ITERS,)), dma((ITERS,)), dma((ITERS, GROUP)), dma((ITERS, GROUP)),
         dma((ITERS,)), dma((ITERS,)), dma((ITERS, rb)), dma((ITERS, rb)),
-        dma((n,)), dma((n,)),
+        dma((1,)), dma((1,)),
     ]
     return pl.pallas_call(
         make_kernel(n, rhs, cols, band),
@@ -396,7 +394,7 @@
         out_specs=(pl.BlockSpec(memory_space=pltpu.VMEM),) * 2,
         scratch_shapes=scratch,
         compiler_params=pltpu.CompilerParams(
-            collective_id=0, has_side_effects=True, vmem_limit_bytes=48 * 1024 * 1024
+            collective_id=0, has_side_effects=True, vmem_limit_bytes=67043328
         ),
     )(b, x, dg, lo, up, z, us, ls)
 

time: 68.4 us -> 58.3 us (0.85)
  local copies, waits for them, and re-layouts: 8.79 us -> 2.83 us
  Pallas kernels: 58.6 us -> 54.7 us
    unnamed x16 -> x2, local copies, waits for them, and re-layouts: 8.79 us -> 2.83 us
    pallas_call x1, Pallas kernels: 58.6 us -> 54.7 us  [body(): pl.pallas_call(make_kernel(n, rhs, cols, band), out_shape=(jax.ShapeDtype...]
where the time goes in v2:
time: 58.3 us; the launch traced here: 58.1 us
  Pallas kernels  54.7 us (94%)
  local copies, waits for them, and re-layouts  2.83 us (5%)
  between operations  0.64 us (1%)
    pallas_call x1, Pallas kernels, body(): pl.pallas_call(make_kernel(n, rhs, cols, band), out_shape=(jax.ShapeDtype...  54.7 us
    unnamed x2, local copies, waits for them, and re-layouts  2.83 us

profile of v2, /device:TPU:0, one launch (start us, length us, event | category | flops | bytes accessed | tf_op | source)
XLA Modules:
  0.0 58.1 jit_solution(13662391096253689687)
XLA Ops:
  0.6 54.7 %shard_map.95 = (f32[32,1024]{1,0:T(8,128)}, f32[3,32]{1,0:T(4,128)}) custom-call(f32[32,1024]{1,0:T(8,128)} %b_hbm.1, f32[32,1024]{1,0:T(8,128)} %x_hbm.1, f32[1024,256]{1,0:T(8,128)} %d_hbm.1, f32[1024,256]{1,0:T(8,128)} %lo_hbm.1, f32[1024,256]{1,0:T(8,128)} %up_hbm.1, bf16[1024,1024]{1,0:T(8,128)(2,1)} %z_hbm.1, bf16[256,1024]{1,0:T(8,128)(2,1)} %us_hbm.1, ...), custom_call_target="tpu_custom_call" | custom-call | tf_op jit(solution)/shard_map/pallas_call | solution.py:387
  55.3 1.6 %copy.12 = f32[32,1024]{1,0:T(8,128)} copy(f32[32,1024]{1,0:T(8,128)} %get-tuple-element.4) | data formatting | bytes 262144
  56.9 1.3 %copy.13 = f32[3,32]{1,0:T(4,128)} copy(f32[3,32]{1,0:T(4,128)} %get-tuple-element.5) | data formatting | bytes 768

commit v3 on v2

--- a/solution.py
+++ b/solution.py
@@ -72,6 +72,20 @@
         has_left = me > 0
         has_right = me < n - 1
 
+        barrier = pltpu.get_barrier_semaphore()
+
+        def greet(k):
+            pl.semaphore_signal(
+                barrier, inc=1, device_id=(lax.rem(me + k, n),), device_id_type=MESH
+            )
+
+        greet(n - 1)
+
+        @pl.loop(0, (n - 1) // 2)
+        def _(i):
+            greet(1 + i)
+            greet(n - 2 - i)
+
         loads = [
             pltpu.make_async_copy(x_hbm, x, in_sem.at[0]),
             pltpu.make_async_copy(ls_hbm.at[:, pl.ds(tail, band)], lg.at[j], in_sem.at[1]),
@@ -86,14 +100,6 @@
         for c in loads:
             c.start()
 
-        barrier = pltpu.get_barrier_semaphore()
-
-        @pl.loop(1, n)
-        def _(k):
-            pl.semaphore_signal(
-                barrier, inc=1, device_id=(lax.rem(me + k, n),), device_id_type=MESH
-            )
-
         @pl.when(me == 0)
         def _():
             halo_l[...] = jnp.zeros_like(halo_l)
@@ -138,12 +144,23 @@
         pl.semaphore_wait(barrier, n - 1)
         halo_start(0)
 
-        l_copies = [rcopy(lg.at[j], lg.at[j], l_send.at[0], l_recv.at[j], partner)]
-        for k in range(1, GROUP // 2):
-            l_copies.append(
-                rcopy(lg.at[j], lg.at[j], l_send.at[k], l_recv.at[j],
-                      base + lax.rem(j + 2 * k, GROUP))
-            )
+        core = lax.rem(j, 2)
+        xflip = j + 2 - 4 * lax.rem(j // 2, 2)
+        yflip = j + 4 - 8 * lax.rem(j // 4, 2)
+        both = xflip + yflip - j
+        relay = (1 - core) * xflip + core * yflip
+        onward = (1 - core) * yflip + core * xflip
+
+        def l_copy(owner, slot, target):
+            return rcopy(lg.at[owner], lg.at[owner], l_send.at[slot], l_recv.at[owner],
+                         base + target)
+
+        buddy = partner - base
+        l_copies = [
+            l_copy(j, 0, buddy),
+            l_copy(j, 1, relay),
+            l_copy(j, 2, onward),
+        ]
         loads[2].wait()
         loads[3].wait()
         u_copy = rcopy(us.at[:, pl.ds(tail, band)], uprev, nb_send.at[0], nb_recv.at[0], right)
@@ -165,6 +182,12 @@
 
         loads[7].wait()
         loads[8].wait()
+
+        def forward(owner, slot, target):
+            c = l_copy(owner, slot, target)
+            c.wait_recv()
+            c.start()
+            l_copies.append(c)
 
         def residual(it):
             sp = [stacked_split(x[:, k * band:(k + 1) * band]) for k in range(blocks)]
@@ -180,6 +203,12 @@
                 if k < blocks - 1:
                     t = t - term(sp[k + 1], 2, k)
                 acc.append(t)
+            if it == 0:
+                l_copy(relay, 0, buddy).wait_recv()
+                for slot, target in ((6, onward), (3, buddy)):
+                    c = l_copy(relay, slot, target)
+                    c.start()
+                    l_copies.append(c)
             halo_wait_recv(it)
             acc[0] = acc[0] - term(stacked_split(halo_l[it]), 0, 0)
             acc[-1] = acc[-1] - term(stacked_split(halo_r[it]), 2, blocks - 1)
@@ -219,13 +248,8 @@
                 loc[:, k * band:(k + 1) * band] = dot(rounded, z[:, k * band:(k + 1) * band])
 
             if it == 0:
-                for k in range(1, GROUP // 2):
-                    owner = lax.rem(j + 2 * k, GROUP)
-                    c = rcopy(lg.at[owner], lg.at[owner], l_send.at[GROUP // 2 - 1 + k],
-                              l_recv.at[owner], partner)
-                    c.wait_recv()
-                    c.start()
-                    l_copies.append(c)
+                for slot, owner in ((4, onward), (5, both)):
+                    forward(owner, slot, buddy)
                 pl.when(has_left)(t_copy.start)
                 for k in range(GROUP // 2):
                     owner = lax.rem(j + 1 - 2 * lax.rem(j, 2) + 2 * k + GROUP, GROUP)

time: 58.3 us -> 57.3 us (0.983)
  Pallas kernels: 54.7 us -> 53.7 us
    pallas_call x1, Pallas kernels: 54.7 us -> 53.7 us  [body(): pl.pallas_call(make_kernel(n, rhs, cols, band), out_shape=(jax.ShapeDtype...]
where the time goes in v3:
time: 57.3 us; the launch traced here: 57.1 us
  Pallas kernels  53.7 us (94%)
  local copies, waits for them, and re-layouts  2.83 us (5%)
  between operations  0.64 us (1%)
    pallas_call x1, Pallas kernels, body(): pl.pallas_call(make_kernel(n, rhs, cols, band), out_shape=(jax.ShapeDtype...  53.7 us
    unnamed x2, local copies, waits for them, and re-layouts  2.83 us

profile of v3, /device:TPU:0, one launch (start us, length us, event | category | flops | bytes accessed | tf_op | source)
XLA Modules:
  0.0 57.1 jit_solution(13184019701437915225)
XLA Ops:
  0.6 53.7 %shard_map.95 = (f32[32,1024]{1,0:T(8,128)}, f32[3,32]{1,0:T(4,128)}) custom-call(f32[32,1024]{1,0:T(8,128)} %b_hbm.1, f32[32,1024]{1,0:T(8,128)} %x_hbm.1, f32[1024,256]{1,0:T(8,128)} %d_hbm.1, f32[1024,256]{1,0:T(8,128)} %lo_hbm.1, f32[1024,256]{1,0:T(8,128)} %up_hbm.1, bf16[1024,1024]{1,0:T(8,128)(2,1)} %z_hbm.1, bf16[256,1024]{1,0:T(8,128)(2,1)} %us_hbm.1, ...), custom_call_target="tpu_custom_call" | custom-call | tf_op jit(solution)/shard_map/pallas_call | solution.py:411
  54.3 1.6 %copy.12 = f32[32,1024]{1,0:T(8,128)} copy(f32[32,1024]{1,0:T(8,128)} %get-tuple-element.4) | data formatting | bytes 262144
  55.9 1.3 %copy.13 = f32[3,32]{1,0:T(4,128)} copy(f32[3,32]{1,0:T(4,128)} %get-tuple-element.5) | data formatting | bytes 768
